TPU v7x, 32 devices: a whole 2x2x4 slice. The times are simulated.
32 devices in a mesh: dp: 4 (over y, core), mp: 8 (over z, x).
Axes of the slice: x: 2, y: 2, z: 4, core: 2. Of those that a mesh axis runs over, the one named last changes fastest.
Arguments:
- tokens: bfloat16 [9216, 1024], P(('dp', 'mp')), may hold values from -6 to 6
- image_ids: int32 [9216], P('dp'), may hold values from 0 to 1, as said below
- lengths: int32 [4, 2], P('dp'), may hold values from 0 to 2304, as said below
- w_qkv: bfloat16 [3, 1024, 1024], P(None, None, 'mp'), may hold values from -0.1875 to 0.1875
- bias_query: float32 [1024], P('mp'), may hold values from -3 to 3
- bias_value: float32 [1024], P('mp'), may hold values from -0.3 to 0.3
- w_out: bfloat16 [1024, 1024], P('mp'), may hold values from -3 to 3
- w_up: bfloat16 [1024, 4096], P(None, 'mp'), may hold values from -0.1875 to 0.1875
- bias_up: float32 [4096], P('mp'), may hold values from -3 to 3
- w_down: bfloat16 [4096, 1024], P('mp'), may hold values from -0.09375 to 0.09375
- out_biases: float32 [2, 1024], replicated, may hold values from -2 to 2
- norm_gain: float32 [2, 1024], replicated, may hold values from 0.25 to 1.75
- norm_bias: float32 [2, 1024], replicated, may hold values from -2 to 2
- cotangent: bfloat16 [9216, 1024], P(('dp', 'mp')), may hold values from -6 to 6
Outputs:
- output: bfloat16 [9216, 1024], P(('dp', 'mp'))
- input_grad: bfloat16 [9216, 1024], P(('dp', 'mp'))
- grad_w_qkv: float32 [3, 1024, 1024], P(None, None, 'mp')
- grad_bias_query: float32 [1024], P('mp')
- grad_bias_value: float32 [1024], P('mp')
- grad_w_out: float32 [1024, 1024], P('mp')
- grad_w_up: float32 [1024, 4096], P(None, 'mp')
- grad_bias_up: float32 [4096], P('mp')
- grad_w_down: float32 [4096, 1024], P('mp')
- grad_out_biases: float32 [2, 1024], replicated
- grad_norm_gain: float32 [2, 1024], replicated
- grad_norm_bias: float32 [2, 1024], replicated
Inputs may be any that keep to these rules, and one draw needn't show every extreme that they name: `image_ids`: within each group of 2304 rows (one group for each index of dp) the image numbers never fall: a group holds either one image over all its rows, or two images of 1152 rows each. lengths[g, k] counts the valid rows at the start of image k of group g: 2304 for an image that fills its group (the second entry is then 0), else 1024. Some group holds an image of 2304 rows.
All inputs are finite; a program needn't handle non-finite values.
Results may differ from a plain program's by a relative error of at most 0.02.
Values may be sent and summed in bfloat16 or wider, within the bound.
A program may use at most 128 MiB of HBM per device.

v0:
```python
import jax
import jax.numpy as jnp
from jax import lax
from jax.sharding import PartitionSpec as P

HEAD_DIM = 64
BLOCK = 768
epsilon = 1e-06


def layer_norm(values, gain_vec, shift_vec):
    row_mean = jnp.mean(values, axis=-1, keepdims=True)
    centered = values - row_mean
    variance = jnp.mean(centered * centered, axis=-1, keepdims=True)
    return centered * lax.rsqrt(variance + epsilon) * gain_vec + shift_vec


def exact_gelu(values):
    return jax.nn.gelu(values, approximate=False)


def valid_rows(image_ids, group_lengths):
    total_rows = image_ids.shape[0]
    row_index = jnp.arange(total_rows, dtype=jnp.int32)
    member = image_ids[:, None] == jnp.arange(2, dtype=jnp.int32)[None, :]
    first_row = jnp.min(jnp.where(member, row_index[:, None], total_rows), axis=0)
    row_start = jnp.sum(jnp.where(member, first_row[None, :], 0), axis=1)
    row_limit = jnp.sum(jnp.where(member, group_lengths[None, :], 0), axis=1)
    return row_index - row_start < row_limit


def allowed_keys(first_query, image_ids, valid_mask):
    total_rows = image_ids.shape[0]
    row_index = jnp.arange(total_rows, dtype=jnp.int32)
    query_rows = first_query + jnp.arange(BLOCK, dtype=jnp.int32)
    query_ids = lax.dynamic_slice_in_dim(image_ids, first_query, BLOCK, 0)
    same_image = (query_ids[:, None] == image_ids[None, :]) & valid_mask[None, :]
    return same_image | (query_rows[:, None] == row_index[None, :])


def block_scores(query_block, keys_all, first_query, image_ids, valid_mask):
    scores = jnp.einsum(
        "qhd,khd->hqk", query_block, keys_all, preferred_element_type=jnp.float32
    ) * HEAD_DIM ** (-0.5)
    allowed = allowed_keys(first_query, image_ids, valid_mask)
    return jnp.where(allowed[None, :, :], scores, -1e30)


def attend_forward(queries, keys_all, values_all, image_ids, valid_mask):

    def one_block(block_number):
        first_query = block_number * BLOCK
        query_block = lax.dynamic_slice_in_dim(queries, first_query, BLOCK, 0)
        scores = block_scores(query_block, keys_all, first_query, image_ids, valid_mask)
        row_max = jnp.max(scores, axis=-1)
        weights = jnp.exp(scores - row_max[:, :, None])
        row_total = jnp.sum(weights, axis=-1)
        probs_low = (weights / row_total[:, :, None]).astype(jnp.bfloat16)
        attended = jnp.einsum(
            "hqk,khd->qhd", probs_low, values_all, preferred_element_type=jnp.float32
        )
        return (attended.astype(jnp.bfloat16), row_max + jnp.log(row_total))

    block_count = queries.shape[0] // BLOCK
    attended, log_totals = lax.map(one_block, jnp.arange(block_count, dtype=jnp.int32))
    return (attended.reshape(queries.shape), log_totals)


def attend_backward(
    queries, keys_all, values_all, log_totals, grad_attended, image_ids, valid_mask
):
    scale_factor = HEAD_DIM ** (-0.5)
    block_count = queries.shape[0] // BLOCK

    def scan_step(totals, block_number):
        key_total, value_total = totals
        first_query = block_number * BLOCK
        query_block = lax.dynamic_slice_in_dim(queries, first_query, BLOCK, 0)
        grad_block = lax.dynamic_slice_in_dim(grad_attended, first_query, BLOCK, 0)
        scores = block_scores(query_block, keys_all, first_query, image_ids, valid_mask)
        probabilities = jnp.exp(scores - log_totals[block_number][:, :, None])
        probs_low = probabilities.astype(jnp.bfloat16)
        value_total = value_total + jnp.einsum(
            "hqk,qhd->khd", probs_low, grad_block, preferred_element_type=jnp.float32
        )
        grad_probs = jnp.einsum(
            "qhd,khd->hqk", grad_block, values_all, preferred_element_type=jnp.float32
        )
        inner_sum = jnp.sum(probabilities * grad_probs, axis=-1, keepdims=True)
        grad_scores = (probabilities * (grad_probs - inner_sum)).astype(jnp.bfloat16)
        grad_query = (
            jnp.einsum("hqk,khd->qhd", grad_scores, keys_all, preferred_element_type=jnp.float32)
            * scale_factor
        )
        key_total = (
            key_total
            + jnp.einsum(
                "hqk,qhd->khd", grad_scores, query_block, preferred_element_type=jnp.float32
            )
            * scale_factor
        )
        return ((key_total, value_total), grad_query.astype(jnp.bfloat16))

    zero_state = jnp.zeros(queries.shape, jnp.float32)
    (key_total, value_total), grad_queries = lax.scan(
        scan_step, (zero_state, zero_state), jnp.arange(block_count, dtype=jnp.int32)
    )
    return (
        grad_queries.reshape(queries.shape),
        key_total.astype(jnp.bfloat16),
        value_total.astype(jnp.bfloat16),
    )


def body(
    tokens,
    image_ids,
    lengths,
    w_qkv,
    bias_query,
    bias_value,
    w_out,
    w_up,
    bias_up,
    w_down,
    out_biases,
    norm_gain,
    norm_bias,
    cotangent,
):
    share_rows = tokens.shape[0]
    local_width = w_qkv.shape[2]
    local_heads = local_width // HEAD_DIM
    total_rows = image_ids.shape[0]
    model_index = lax.axis_index("mp")
    valid_mask = valid_rows(image_ids, lengths[0])
    own_valid = lax.dynamic_slice_in_dim(
        valid_mask.astype(jnp.float32), model_index * share_rows, share_rows, 0
    )

    def split_heads(matrix):
        return matrix.reshape(total_rows, local_heads, HEAD_DIM)

    inputs_f = tokens.astype(jnp.float32)
    normed_one = layer_norm(inputs_f, norm_gain[0], norm_bias[0]).astype(jnp.bfloat16)
    gathered_one = lax.all_gather(normed_one, "mp", axis=0, tiled=True)
    projected = jnp.einsum("rd,tde->tre", gathered_one, w_qkv, preferred_element_type=jnp.float32)
    queries = split_heads((projected[0] + bias_query).astype(jnp.bfloat16))
    keys_all = split_heads(projected[1].astype(jnp.bfloat16))
    values_all = split_heads((projected[2] + bias_value).astype(jnp.bfloat16))
    attended, log_totals = attend_forward(queries, keys_all, values_all, image_ids, valid_mask)
    attended = attended.reshape(total_rows, local_width)
    hidden_one = (
        inputs_f
        + lax.psum_scatter(
            jnp.dot(attended, w_out, preferred_element_type=jnp.float32).astype(jnp.bfloat16),
            "mp",
            scatter_dimension=0,
            tiled=True,
        ).astype(jnp.float32)
        + out_biases[0]
    )
    normed_two = layer_norm(hidden_one, norm_gain[1], norm_bias[1]).astype(jnp.bfloat16)
    gathered_two = lax.all_gather(normed_two, "mp", axis=0, tiled=True)
    pre_act = jnp.dot(gathered_two, w_up, preferred_element_type=jnp.float32) + bias_up
    activated = exact_gelu(pre_act).astype(jnp.bfloat16)
    output_full = (
        hidden_one
        + lax.psum_scatter(
            jnp.dot(activated, w_down, preferred_element_type=jnp.float32).astype(jnp.bfloat16),
            "mp",
            scatter_dimension=0,
            tiled=True,
        ).astype(jnp.float32)
        + out_biases[1]
    )
    kept_state = (
        gathered_one,
        queries,
        keys_all,
        values_all,
        log_totals,
        attended,
        hidden_one,
        gathered_two,
        pre_act,
        activated,
    )
    output_full, kept_state = (output_full, kept_state)
    (
        gathered_one,
        queries,
        keys_all,
        values_all,
        log_totals,
        attended,
        hidden_one,
        gathered_two,
        pre_act,
        activated,
    ) = kept_state
    tokens_f = tokens.astype(jnp.float32)
    grad_out = cotangent.astype(jnp.float32) * own_valid[:, None]
    grad_mlp = lax.all_gather(grad_out.astype(jnp.bfloat16), "mp", axis=0, tiled=True)
    grad_w_down = jnp.einsum("rf,rd->fd", activated, grad_mlp, preferred_element_type=jnp.float32)
    grad_act = jnp.einsum("rd,fd->rf", grad_mlp, w_down, preferred_element_type=jnp.float32)
    _, gelu_back = jax.vjp(exact_gelu, pre_act)
    grad_pre = gelu_back(grad_act)[0].astype(jnp.bfloat16)
    grad_w_up = jnp.einsum("rd,rf->df", gathered_two, grad_pre, preferred_element_type=jnp.float32)
    grad_bias_up = jnp.sum(grad_pre, axis=0, dtype=jnp.float32)
    grad_normed_two = lax.psum_scatter(
        jnp.einsum("rf,df->rd", grad_pre, w_up, preferred_element_type=jnp.float32).astype(
            jnp.bfloat16
        ),
        "mp",
        scatter_dimension=0,
        tiled=True,
    ).astype(jnp.float32)
    _, norm_two_back = jax.vjp(layer_norm, hidden_one, norm_gain[1], norm_bias[1])
    grad_from_two, gain_two, shift_two = norm_two_back(grad_normed_two)
    grad_hidden = grad_out + grad_from_two
    grad_proj = lax.all_gather(grad_hidden.astype(jnp.bfloat16), "mp", axis=0, tiled=True)
    grad_w_out = jnp.einsum("re,rd->ed", attended, grad_proj, preferred_element_type=jnp.float32)
    grad_attended = jnp.einsum(
        "rd,ed->re", grad_proj, w_out, preferred_element_type=jnp.float32
    ).astype(jnp.bfloat16)
    grad_queries, grad_keys, grad_values = attend_backward(
        queries, keys_all, values_all, log_totals, split_heads(grad_attended), image_ids, valid_mask
    )
    grad_stack = jnp.stack(
        [
            grad_queries.reshape(total_rows, local_width),
            grad_keys.reshape(total_rows, local_width),
            grad_values.reshape(total_rows, local_width),
        ]
    )
    grad_w_qkv = jnp.einsum(
        "rd,tre->tde", gathered_one, grad_stack, preferred_element_type=jnp.float32
    )
    grad_bias_query = jnp.sum(grad_stack[0], axis=0, dtype=jnp.float32)
    grad_bias_value = jnp.sum(grad_stack[2], axis=0, dtype=jnp.float32)
    grad_normed_one = lax.psum_scatter(
        jnp.einsum("tre,tde->rd", grad_stack, w_qkv, preferred_element_type=jnp.float32).astype(
            jnp.bfloat16
        ),
        "mp",
        scatter_dimension=0,
        tiled=True,
    ).astype(jnp.float32)
    _, norm_one_back = jax.vjp(layer_norm, tokens_f, norm_gain[0], norm_bias[0])
    grad_from_one, gain_one, shift_one = norm_one_back(grad_normed_one)
    input_grad = (grad_hidden + grad_from_one).astype(jnp.bfloat16)
    grad_norm_gain, grad_norm_bias, grad_out_biases = lax.psum(
        (
            jnp.stack([gain_one, gain_two]),
            jnp.stack([shift_one, shift_two]),
            jnp.stack([jnp.sum(grad_hidden, axis=0), jnp.sum(grad_out, axis=0)]),
        ),
        ("dp", "mp"),
    )
    (
        grad_w_qkv,
        grad_bias_query,
        grad_bias_value,
        grad_w_out,
        grad_w_up,
        grad_bias_up,
        grad_w_down,
    ) = (
        lax.psum(grad_w_qkv.astype(jnp.bfloat16), "dp").astype(jnp.float32),
        lax.psum(grad_bias_query.astype(jnp.bfloat16), "dp").astype(jnp.float32),
        lax.psum(grad_bias_value.astype(jnp.bfloat16), "dp").astype(jnp.float32),
        lax.psum(grad_w_out.astype(jnp.bfloat16), "dp").astype(jnp.float32),
        lax.psum(grad_w_up.astype(jnp.bfloat16), "dp").astype(jnp.float32),
        lax.psum(grad_bias_up.astype(jnp.bfloat16), "dp").astype(jnp.float32),
        lax.psum(grad_w_down.astype(jnp.bfloat16), "dp").astype(jnp.float32),
    )
    return (
        output_full.astype(jnp.bfloat16),
        input_grad,
        grad_w_qkv,
        grad_bias_query,
        grad_bias_value,
        grad_w_out,
        grad_w_up,
        grad_bias_up,
        grad_w_down,
        grad_out_biases,
        grad_norm_gain,
        grad_norm_bias,
    )


def solution(mesh):
    in_specs = (
        P(("dp", "mp"), None),
        P("dp"),
        P("dp", None),
        P(None, None, "mp"),
        P("mp"),
        P("mp"),
        P("mp", None),
        P(None, "mp"),
        P("mp"),
        P("mp", None),
        P(),
        P(),
        P(),
        P(("dp", "mp"), None),
    )
    out_specs = (
        P(("dp", "mp"), None),
        P(("dp", "mp"), None),
        P(None, None, "mp"),
        P("mp"),
        P("mp"),
        P("mp", None),
        P(None, "mp"),
        P("mp"),
        P("mp", None),
        P(),
        P(),
        P(),
    )
    return jax.shard_map(body, mesh=mesh, in_specs=in_specs, out_specs=out_specs, check_vma=False)
```

profile of v0, /device:TPU:0, one launch (start us, length us, event | category | flops | bytes accessed | tf_op | source)
XLA Modules:
  0.0 1075.9 jit_solution(2535776291158847635)
XLA Ops:
  16.4 81.4 %all-gather.5.cloned.1.call-done = bf16[2304,1024]{1,0:T(8,128)(2,1)} async-done(((bf16[288,1024]{1,0:T(8,128)(2,1)}), bf16[2304,1024]{1,0:T(8,128)(2,1)}) %all-gather.5.cloned.1.call-update) | async-done | bytes 4718608 | tf_op jit(solution)/shard_map/all_gather | solution.py:146
  97.8 4.4 fusion.83
  102.7 45.9 %while.27 = (s32[]{:T(128)}, bf16[3,768,2,64]{1,3,2,0:T(8,128)(2,1)S(1)}, f32[3,2,768]{2,1,0:T(2,128)S(1)}, s32[3]{0:T(128)S(1)}, s32[2304]{0:T(1024)S(1)}, /*in...) while((s32[]{:T(128)}, ...), condition=%wide.region_8.9_spmd, body=%wide.region_5.8_spmd.sunk | while | flops 955612416 | bytes 51194320 | solution.py:65
  106.3 3.3 fusion.135
  109.7 4.1 fusion.136
  113.8 4.2 fusion.137
  121.7 3.3 fusion.135
  125.0 4.1 fusion.136
  129.1 4.1 fusion.137
  137.0 3.3 fusion.135
  140.3 4.1 fusion.136
  144.4 4.1 fusion.137
  149.7 3.6 convolution_convert_fusion.2
  154.0 93.5 %reduce-scatter.5.cloned.1.call-done = bf16[288,1024]{1,0:T(8,128)(2,1)} async-done(((bf16[2304,1024]{1,0:T(8,128)(2,1)}), bf16[288,1024]{1,0:T(8,128)(2,1)}) %reduce-scatter.5.cloned.1.call-update) | async-done | bytes 589840 | tf_op jit(solution)/shard_map/reduce_scatter | solution.py:155
  253.9 76.8 %all-gather.7.cloned.1.call-done = bf16[2304,1024]{1,0:T(8,128)(2,1)} async-done(((bf16[288,1024]{1,0:T(8,128)(2,1)}), bf16[2304,1024]{1,0:T(8,128)(2,1)}) %all-gather.7.cloned.1.call-update) | async-done | bytes 4718608 | tf_op jit(solution)/shard_map/all_gather | solution.py:164
  330.7 7.4 convolution_add_fusion
  338.1 73.0 %all-gather.9.cloned.1.call-done = bf16[2304,1024]{1,0:T(8,128)(2,1)} async-done(((bf16[288,1024]{1,0:T(8,128)(2,1)}), bf16[2304,1024]{1,0:T(8,128)(2,1)}) %all-gather.9.cloned.1.call-update) | async-done | bytes 4718608 | tf_op jit(solution)/shard_map/all_gather | solution.py:204
  411.0 17.0 %fusion.76 = (bf16[512]{0:T(512)(128)(2,1)}, bf16[2304,512]{1,0:T(8,128)(2,1)S(1)}, f32[2304,512]{1,0:T(8,128)}) fusion(f32[2304,512]{1,0:T(8,128)} %convolution_add_fusion, bf16[2304,1024]{1,0:T(8,128)(2,1)} %all-gather.9.cloned.1.call-done, bf16[512,1024]{1,0:T(8,128)(2,1)S(1)} %copy-done), kind=kOutput, calls=%fused_computation.140 | convolution fusion | flops 2502032896 | bytes 17564672 | tf_op jit(solution)/shard_map/rd,fd->rf/dot_general | solution.py:206
  429.5 4.4 convolution_convert_fusion
  434.0 5.0 multiply_convert_fusion.1
  440.4 4.2 convolution_convert_fusion.1
  445.0 83.2 %reduce-scatter.9.cloned.1.call-done = bf16[288,1024]{1,0:T(8,128)(2,1)} async-done(((bf16[2304,1024]{1,0:T(8,128)(2,1)}), bf16[288,1024]{1,0:T(8,128)(2,1)}) %reduce-scatter.9.cloned.1.call-update) | async-done | bytes 589840 | tf_op jit(solution)/shard_map/reduce_scatter | solution.py:211
  532.9 94.1 %reduce-scatter.7.cloned.1.call-done = bf16[288,1024]{1,0:T(8,128)(2,1)} async-done(((bf16[2304,1024]{1,0:T(8,128)(2,1)}), bf16[288,1024]{1,0:T(8,128)(2,1)}) %reduce-scatter.7.cloned.1.call-update) | async-done | bytes 589840 | tf_op jit(solution)/shard_map/reduce_scatter | solution.py:169
  626.9 3.4 fusion.75
  632.4 6.8 convolution_convert_fusion.5
  639.2 6.3 convolution_convert_fusion.4
  645.6 65.8 %all-gather.11.cloned.1.call-done = bf16[2304,1024]{1,0:T(8,128)(2,1)} async-done(((bf16[288,1024]{1,0:T(8,128)(2,1)}), bf16[2304,1024]{1,0:T(8,128)(2,1)}) %all-gather.11.cloned.1.call-update) | async-done | bytes 4718608 | tf_op jit(solution)/shard_map/all_gather | solution.py:222
  711.4 4.8 convolution_convert_fusion.3
  717.1 124.3 %while.28 = (s32[]{:T(128)}, f32[2304,2,64]{0,2,1:T(8,128)S(1)}, f32[2304,2,64]{0,2,1:T(8,128)}, bf16[3,768,2,64]{1,3,2,0:T(8,128)(2,1)}, s32[3]{0:T(128)S(1)}, ...) while((s32[]{:T(128)}, f32[2304,2,64]{0,2,1:T(8,128)S(1)}, ...), condition=%wide.region_18.19_spmd.clone, body=%wide.region_16.18_spmd.clone.sunk | while | flops 2305522944 | bytes 154985072 | solution.py:105
  723.1 8.0 fusion.147
  731.1 8.4 multiply_reduce_fusion.3
  739.5 8.9 multiply_convert_fusion.3
  750.9 6.4 fusion.151
  764.4 8.0 fusion.147
  772.4 8.4 multiply_reduce_fusion.3
  780.8 8.9 multiply_convert_fusion.3
  792.2 6.4 fusion.151
  805.7 8.0 fusion.147
  813.7 8.4 multiply_reduce_fusion.3
  822.1 8.9 multiply_convert_fusion.3
  833.5 6.4 fusion.151
  847.6 4.1 convolution_convert_fusion.6
  851.7 5.2 fusion.54
  858.2 5.4 bitcast_convert_fusion
  864.7 6.5 all-reduce.1
  872.8 51.4 %all-reduce.5.cloned.1.call-done = (bf16[3,1024,128]{1,2,0:T(8,128)(2,1)}, bf16[128,1024]{1,0:T(8,128)(2,1)}, bf16[1024,512]{1,0:T(8,128)(2,1)}, bf16[512,1024]{1,0:T(8,128)(2,1)}) async-done(((bf16[3,1024,128]{1,2,0:T(8,128)(2,1)}, bf16[128,1024]{1,0:T(8,128)(2,1)}, bf16[1024,512]{1,0:T(8,128)(2,1)}, bf16[512,1024]{1,0:T(8,128)(2,1)}), (bf16[3,1024,128]{1,2,0:T(8,128)(2,1)}, bf16[128,1024]{1,0:T(8,128)(2,1)}, ...) | async-done | bytes 3145744 | tf_op jit(solution)/shard_map/psum | solution.py:270
  931.9 91.7 %reduce-scatter.11.cloned.1.call-done = bf16[288,1024]{1,0:T(8,128)(2,1)} async-done(((bf16[2304,1024]{1,0:T(8,128)(2,1)}), bf16[288,1024]{1,0:T(8,128)(2,1)}) %reduce-scatter.11.cloned.1.call-update) | async-done | bytes 589840 | tf_op jit(solution)/shard_map/reduce_scatter | solution.py:242
  1027.1 40.8 %all-reduce = (f32[2,1024]{1,0:T(2,128)}, f32[2,1024]{1,0:T(2,128)}, f32[2,1024]{1,0:T(2,128)}) all-reduce(f32[2,1024]{1,0:T(2,128)S(1)} %pad_maximum_fusion.3, f32[2,1024]{1,0:T(2,128)S(1)} %pad_maximum_fusion.4, f32[2,1024]{1,0:T(2,128)S(1)} %pad_maximum_fusion.5), channel_id=1, replica_groups=mesh['dp'=4,'mp'=8] {'dp','mp'}, use_global_device_ids=true, to_apply=%region_34.35 | all-reduce | flops 6144 | bytes 49152 | tf_op jit(solution)/shard_map/psum | solution.py:253
  (234 shorter events, 80.8 us)
Async XLA Ops:
  7.2 403.9 %copy-start = (bf16[512,1024]{1,0:T(8,128)(2,1)S(1)}, bf16[512,1024]{1,0:T(8,128)(2,1)}, u32[]{:S(2)}) copy-start(bf16[512,1024]{1,0:T(8,128)(2,1)} %param.27) | copy-start | bytes 3145732
  7.2 8.4 copy-start.50
  7.2 8.5 copy-start.51
  7.2 8.6 copy-start.23
  7.2 8.9 copy-start.18
  7.2 9.0 copy-start.47
  7.2 90.5 %all-gather.5.cloned.1.call-start = ((), (), s32[]{:S(2)}) async-start(), calls=%async_computation.4 | async-start | bytes 5308416 | tf_op jit(solution)/shard_map/all_gather | solution.py:146
  8.7 93.5 %copy-start.34 = (f32[288]{0:T(512)}, f32[288]{0:T(512)S(1)}, u32[]{:S(2)}) copy-start(f32[288]{0:T(512)S(1)} %broadcast_multiply_fusion.1) | copy-start | bytes 3460
  10.6 5.6 copy-start.36
  12.0 90.1 %copy-start.31 = (f32[1,1024]{1,0:T(1,128)}, f32[1,1024]{1,0:T(1,128)S(1)}, u32[]{:S(2)}) copy-start(f32[1,1024]{1,0:T(1,128)S(1)} %get-tuple-element.283) | copy-start | bytes 12292
  15.6 231.9 %reduce-scatter.5.cloned.1.call-start = ((), (), s32[]{:S(2)}) async-start(), calls=%async_computation.5 | async-start | bytes 5308416 | tf_op jit(solution)/shard_map/reduce_scatter | solution.py:155
  148.6 4.7 copy-start.9
  153.3 94.2 %copy-start.3 = (bf16[288,1024]{1,0:T(8,128)(2,1)S(1)}, bf16[288,1024]{1,0:T(8,128)(2,1)}, u32[]{:S(2)}) copy-start(bf16[288,1024]{1,0:T(8,128)(2,1)} %param.18) | copy-start | bytes 1769476
  153.3 97.1 %copy-start.33 = (f32[1,1024]{1,0:T(1,128)S(1)}, f32[1,1024]{1,0:T(1,128)}, u32[]{:S(2)}) copy-start(f32[1,1024]{1,0:T(1,128)} %get-tuple-element.284) | copy-start | bytes 12292
  153.3 97.1 %copy-start.44 = (f32[1,1024]{1,0:T(1,128)S(1)}, f32[1,1024]{1,0:T(1,128)}, u32[]{:S(2)}) copy-start(f32[1,1024]{1,0:T(1,128)} %get-tuple-element.286) | copy-start | bytes 12292
  153.4 177.4 %all-gather.7.cloned.1.call-start = ((), (), s32[]{:S(2)}) async-start(), calls=%async_computation.6 | async-start | bytes 5308416 | tf_op jit(solution)/shard_map/all_gather | solution.py:164
  250.4 80.3 %copy-start.49 = (f32[512]{0:T(512)S(1)}, f32[512]{0:T(512)}, u32[]{:S(2)}) copy-start(f32[512]{0:T(512)} %param.26) | copy-start | bytes 6148
  251.6 159.4 %all-gather.9.cloned.1.call-start = ((), (), s32[]{:S(2)}) async-start(), calls=%async_computation.8 | async-start | bytes 5308416 | tf_op jit(solution)/shard_map/all_gather | solution.py:204
  253.8 274.3 %reduce-scatter.9.cloned.1.call-start = ((), (), s32[]{:S(2)}) async-start(), calls=%async_computation.9 | async-start | bytes 5308416 | tf_op jit(solution)/shard_map/reduce_scatter | solution.py:211
  411.0 18.4 %copy-start.48 = (bf16[1024,512]{1,0:T(8,128)(2,1)S(1)}, bf16[1024,512]{1,0:T(8,128)(2,1)}, u32[]{:S(2)}) copy-start(bf16[1024,512]{1,0:T(8,128)(2,1)} %param.25) | copy-start | bytes 3145732
  433.9 193.0 %reduce-scatter.7.cloned.1.call-start = ((), (), s32[]{:S(2)}) async-start(), calls=%async_computation.7 | async-start | bytes 5308416 | tf_op jit(solution)/shard_map/reduce_scatter | solution.py:169
  444.7 266.7 %all-gather.11.cloned.1.call-start = ((), (), s32[]{:S(2)}) async-start(), calls=%async_computation.10 | async-start | bytes 5308416 | tf_op jit(solution)/shard_map/all_gather | solution.py:222
  528.1 98.8 %copy-start.15 = (bf16[288,1024]{1,0:T(8,128)(2,1)S(1)}, bf16[288,1024]{1,0:T(8,128)(2,1)}, u32[]{:S(2)}) copy-start(bf16[288,1024]{1,0:T(8,128)(2,1)} %reduce-scatter.9.cloned.1.call-done) | copy-start | bytes 1769476
  632.3 291.8 %all-reduce.5.cloned.1.call-start = ((), (), s32[]{:S(2)}) async-start(), calls=%async_computation.12 | async-start | bytes 6291456 | tf_op jit(solution)/shard_map/psum | solution.py:270
  632.4 6.9 copy-start.20
  639.2 72.2 %copy-start.30 = (bf16[128,1024]{1,0:T(8,128)(2,1)S(1)}, bf16[128,1024]{1,0:T(8,128)(2,1)}, u32[]{:S(2)}) copy-start(bf16[128,1024]{1,0:T(8,128)(2,1)} %param.24) | copy-start | bytes 786436
  645.6 71.5 %copy-start.10 = (bf16[2304,2,64]{0,2,1:T(8,128)(2,1)S(1)}, bf16[2304,2,64]{0,2,1:T(8,128)(2,1)}, u32[]{:S(2)}) copy-start(bf16[2304,2,64]{0,2,1:T(8,128)(2,1)} %copy-done.9) | copy-start | bytes 1769476
  739.5 8.9 copy-start.5
  750.9 6.4 copy-start.6
  750.9 6.4 copy-start.2
  780.8 8.9 copy-start.5
  792.2 6.4 copy-start.6
  792.2 6.4 copy-start.2
  822.1 8.9 copy-start.5
  833.5 6.4 copy-start.6
  833.5 6.4 copy-start.2
  857.0 166.6 %reduce-scatter.11.cloned.1.call-start = ((), (), s32[]{:S(2)}) async-start(), calls=%async_computation.11 | async-start | bytes 5308416 | tf_op jit(solution)/shard_map/reduce_scatter | solution.py:242
  924.1 4.5 copy-start.22
  930.3 93.3 %copy-start.4 = (bf16[288,1024]{1,0:T(8,128)(2,1)S(1)}, bf16[288,1024]{1,0:T(8,128)(2,1)}, u32[]{:S(2)}) copy-start(bf16[288,1024]{1,0:T(8,128)(2,1)} %param.18) | copy-start | bytes 1769476
  930.3 93.3 %copy-start.32 = (f32[1,1024]{1,0:T(1,128)S(1)}, f32[1,1024]{1,0:T(1,128)}, u32[]{:S(2)}) copy-start(f32[1,1024]{1,0:T(1,128)} %copy-done.31) | copy-start | bytes 12292
  930.3 93.3 %copy-start.35 = (f32[288]{0:T(512)S(1)}, f32[288]{0:T(512)}, u32[]{:S(2)}) copy-start(f32[288]{0:T(512)} %copy-done.34) | copy-start | bytes 3460
  930.3 95.0 %copy-start.39 = (f32[288]{0:T(512)S(1)}, f32[288]{0:T(512)}, u32[]{:S(2)}) copy-start(f32[288]{0:T(512)} %copy-done.38) | copy-start | bytes 3460
  930.3 95.0 %copy-start.37 = (f32[288]{0:T(512)S(1)}, f32[288]{0:T(512)}, u32[]{:S(2)}) copy-start(f32[288]{0:T(512)} %copy-done.36) | copy-start | bytes 3460
  930.3 96.8 %copy-start.40 = (f32[1024]{0:T(1024)S(1)}, f32[1024]{0:T(1024)}, u32[]{:S(2)}) copy-start(f32[1024]{0:T(1024)} %get-tuple-element.210) | copy-start | bytes 12292
  930.3 96.8 %copy-start.41 = (f32[1024]{0:T(1024)S(1)}, f32[1024]{0:T(1024)}, u32[]{:S(2)}) copy-start(f32[1024]{0:T(1024)} %get-tuple-element.204) | copy-start | bytes 12292
  930.3 137.6 %copy-start.12 = (f32[288,1024]{1,0:T(8,128)S(1)}, f32[288,1024]{1,0:T(8,128)}, u32[]{:S(2)}) copy-start(f32[288,1024]{1,0:T(8,128)} %copy-done.11) | copy-start | bytes 3538948
  1023.6 44.3 %copy-start.17 = (bf16[288,1024]{1,0:T(8,128)(2,1)S(1)}, bf16[288,1024]{1,0:T(8,128)(2,1)}, u32[]{:S(2)}) copy-start(bf16[288,1024]{1,0:T(8,128)(2,1)} %reduce-scatter.11.cloned.1.call-done) | copy-start | bytes 1769476
  1023.6 45.6 %copy-start.1 = (bf16[512,1024]{1,0:T(8,128)(2,1)S(1)}, bf16[512,1024]{1,0:T(8,128)(2,1)}, u32[]{:S(2)}) copy-start(bf16[512,1024]{1,0:T(8,128)(2,1)} %param.27) | copy-start | bytes 3145732
  (20 other events, 44.1 us)
Sparse Core Ops, SparseCore 0:
  15.7 82.0 all-gather.4
  153.5 94.0 reduce-scatter.4
  251.7 78.9 all-gather.6
  333.3 77.6 all-gather.8
  434.1 94.0 reduce-scatter.8
  531.6 95.2 reduce-scatter.6
  632.4 78.9 all-gather.10
  857.1 66.9 all-reduce.4
  927.8 95.7 reduce-scatter.10
where the time goes:
time: 1090 us; the launch traced here: 1080 us
  waiting for transfers between devices  711 us (65%)
  matrix products  176 us (16%)
  other arithmetic  91.3 us (8%)
  blocking collectives  47.2 us (4%)
  local copies, waits for them, and re-layouts  24.3 us (2%)
  between operations  14.6 us (1%)
    reduce_scatter x1, waiting for transfers between devices, body(): lax.psum_scatter(jnp.dot(activated, w_down, preferred_element_type=jnp.fl...  94.1 us
    reduce_scatter x1, waiting for transfers between devices, body(): lax.psum_scatter(jnp.dot(attended, w_out, preferred_element_type=jnp.floa...  93.5 us
    reduce_scatter x1, waiting for transfers between devices, body(): lax.psum_scatter(jnp.einsum('tre,tde->rd', grad_stack, w_qkv, preferred_e...  91.7 us
    reduce_scatter x1, waiting for transfers between devices, body(): lax.psum_scatter(jnp.einsum('rf,df->rd', grad_pre, w_up, preferred_elemen...  83.2 us
    all_gather x1, waiting for transfers between devices, body(): gathered_one = lax.all_gather(normed_one, 'mp', axis=0, tiled=True)  81.4 us
    all_gather x1, waiting for transfers between devices, body(): gathered_two = lax.all_gather(normed_two, 'mp', axis=0, tiled=True)  76.8 us
    all_gather x1, waiting for transfers between devices, body(): lax.all_gather(grad_out.astype(jnp.bfloat16), 'mp', axis=0, tiled=True)  73 us
    all_gather x1, waiting for transfers between devices, body(): lax.all_gather(grad_hidden.astype(jnp.bfloat16), 'mp', axis=0, tiled=True)  65.8 us
  transfers between devices with their start and end apart: 9, of which 9 were waited for; matrix products, arithmetic and copies ran while one was open for 5% of the time, Pallas kernels for 0%

commit v1 on v0

--- a/solution.py
+++ b/solution.py
@@ -267,7 +267,7 @@
         grad_bias_up,
         grad_w_down,
     ) = (
-        lax.psum(grad_w_qkv.astype(jnp.bfloat16), "dp").astype(jnp.float32),
+        jnp.sum(lax.all_gather(grad_w_qkv.astype(jnp.bfloat16), "dp"), axis=0).astype(jnp.float32),
         lax.psum(grad_bias_query.astype(jnp.bfloat16), "dp").astype(jnp.float32),
         lax.psum(grad_bias_value.astype(jnp.bfloat16), "dp").astype(jnp.float32),
         lax.psum(grad_w_out.astype(jnp.bfloat16), "dp").astype(jnp.float32),

time: 1090 us -> 1050 us (0.963)
  waiting for transfers between devices: 711 us -> 666 us
    psum x1, waiting for transfers between devices: 51.4 us -> 0.01 us  [body(): lax.psum(grad_w_out.astype(jnp.bfloat16), 'dp').astype(jnp.float32)]
  transfers between devices with their start and end apart: 9 -> 10, of which waited for: 9 -> 9; matrix products, arithmetic and copies ran while one was open for 5% -> 19% of each run, Pallas kernels for 0% -> 0%
where the time goes in v1:
time: 1050 us; the launch traced here: 1040 us
  waiting for transfers between devices  666 us (63%)
  matrix products  176 us (17%)
  other arithmetic  95.4 us (9%)
  blocking collectives  47.3 us (5%)
  local copies, waits for them, and re-layouts  27.1 us (3%)
  between operations  14.9 us (1%)
  loops' own time  10.5 us (1%)
    reduce_scatter x1, waiting for transfers between devices, body(): lax.psum_scatter(jnp.dot(activated, w_down, preferred_element_type=jnp.fl...  94.1 us
    reduce_scatter x1, waiting for transfers between devices, body(): lax.psum_scatter(jnp.dot(attended, w_out, preferred_element_type=jnp.floa...  93.5 us
    reduce_scatter x1, waiting for transfers between devices, body(): lax.psum_scatter(jnp.einsum('tre,tde->rd', grad_stack, w_qkv, preferred_e...  92.7 us
    reduce_scatter x1, waiting for transfers between devices, body(): lax.psum_scatter(jnp.einsum('rf,df->rd', grad_pre, w_up, preferred_elemen...  83.1 us
    all_gather x1, waiting for transfers between devices, body(): gathered_one = lax.all_gather(normed_one, 'mp', axis=0, tiled=True)  81.4 us
    all_gather x1, waiting for transfers between devices, body(): gathered_two = lax.all_gather(normed_two, 'mp', axis=0, tiled=True)  76.8 us
    all_gather x1, waiting for transfers between devices, body(): lax.all_gather(grad_out.astype(jnp.bfloat16), 'mp', axis=0, tiled=True)  72.9 us
    all_gather x1, waiting for transfers between devices, body(): lax.all_gather(grad_hidden.astype(jnp.bfloat16), 'mp', axis=0, tiled=True)  65.8 us
  transfers between devices with their start and end apart: 10, of which 9 were waited for; matrix products, arithmetic and copies ran while one was open for 19% of the time, Pallas kernels for 0%

profile of v1, /device:TPU:0, one launch (start us, length us, event | category | flops | bytes accessed | tf_op | source)
XLA Modules:
  0.0 1038.8 jit_solution(3975734697100195690)
XLA Ops:
  16.4 81.4 %all-gather.7.cloned.1.call-done = bf16[2304,1024]{1,0:T(8,128)(2,1)} async-done(((bf16[288,1024]{1,0:T(8,128)(2,1)}), bf16[2304,1024]{1,0:T(8,128)(2,1)}) %all-gather.7.cloned.1.call-update) | async-done | bytes 4718608 | tf_op jit(solution)/shard_map/all_gather | solution.py:146
  97.8 4.4 fusion.83
  102.7 45.9 %while.27 = (s32[]{:T(128)}, bf16[3,768,2,64]{1,3,2,0:T(8,128)(2,1)S(1)}, f32[3,2,768]{2,1,0:T(2,128)S(1)}, s32[3]{0:T(128)S(1)}, s32[2304]{0:T(1024)S(1)}, /*in...) while((s32[]{:T(128)}, ...), condition=%wide.region_8.9_spmd, body=%wide.region_5.8_spmd.sunk | while | flops 955612416 | bytes 51194320 | solution.py:65
  106.4 3.3 fusion.135
  109.7 4.1 fusion.136
  113.8 4.2 fusion.137
  121.7 3.3 fusion.135
  125.0 4.1 fusion.136
  129.1 4.1 fusion.137
  137.0 3.3 fusion.135
  140.3 4.1 fusion.136
  144.4 4.1 fusion.137
  149.8 3.5 convolution_convert_fusion.2
  154.0 93.5 %reduce-scatter.5.cloned.1.call-done = bf16[288,1024]{1,0:T(8,128)(2,1)} async-done(((bf16[2304,1024]{1,0:T(8,128)(2,1)}), bf16[288,1024]{1,0:T(8,128)(2,1)}) %reduce-scatter.5.cloned.1.call-update) | async-done | bytes 589840 | tf_op jit(solution)/shard_map/reduce_scatter | solution.py:155
  253.8 76.8 %all-gather.9.cloned.1.call-done = bf16[2304,1024]{1,0:T(8,128)(2,1)} async-done(((bf16[288,1024]{1,0:T(8,128)(2,1)}), bf16[2304,1024]{1,0:T(8,128)(2,1)}) %all-gather.9.cloned.1.call-update) | async-done | bytes 4718608 | tf_op jit(solution)/shard_map/all_gather | solution.py:164
  330.7 7.4 convolution_add_fusion
  338.1 72.9 %all-gather.11.cloned.1.call-done = bf16[2304,1024]{1,0:T(8,128)(2,1)} async-done(((bf16[288,1024]{1,0:T(8,128)(2,1)}), bf16[2304,1024]{1,0:T(8,128)(2,1)}) %all-gather.11.cloned.1.call-update) | async-done | bytes 4718608 | tf_op jit(solution)/shard_map/all_gather | solution.py:204
  411.0 17.1 %fusion.76 = (bf16[512]{0:T(512)(128)(2,1)}, bf16[2304,512]{1,0:T(8,128)(2,1)S(1)}, f32[2304,512]{1,0:T(8,128)}) fusion(f32[2304,512]{1,0:T(8,128)} %convolution_add_fusion, bf16[2304,1024]{1,0:T(8,128)(2,1)} %all-gather.11.cloned.1.call-done, bf16[512,1024]{1,0:T(8,128)(2,1)S(1)} %copy-done), kind=kOutput, calls=%fused_computation.140 | convolution fusion | flops 2502032896 | bytes 17564672 | tf_op jit(solution)/shard_map/rd,fd->rf/dot_general | solution.py:206
  429.5 4.4 convolution_convert_fusion
  434.0 5.0 multiply_convert_fusion.1
  440.4 4.3 convolution_convert_fusion.1
  445.0 83.1 %reduce-scatter.9.cloned.1.call-done = bf16[288,1024]{1,0:T(8,128)(2,1)} async-done(((bf16[2304,1024]{1,0:T(8,128)(2,1)}), bf16[288,1024]{1,0:T(8,128)(2,1)}) %reduce-scatter.9.cloned.1.call-update) | async-done | bytes 589840 | tf_op jit(solution)/shard_map/reduce_scatter | solution.py:211
  532.8 94.1 %reduce-scatter.7.cloned.1.call-done = bf16[288,1024]{1,0:T(8,128)(2,1)} async-done(((bf16[2304,1024]{1,0:T(8,128)(2,1)}), bf16[288,1024]{1,0:T(8,128)(2,1)}) %reduce-scatter.7.cloned.1.call-update) | async-done | bytes 589840 | tf_op jit(solution)/shard_map/reduce_scatter | solution.py:169
  626.9 3.4 fusion.75
  632.4 6.8 convolution_convert_fusion.5
  639.2 6.3 convolution_convert_fusion.4
  645.6 65.8 %all-gather.13.cloned.1.call-done = bf16[2304,1024]{1,0:T(8,128)(2,1)} async-done(((bf16[288,1024]{1,0:T(8,128)(2,1)}), bf16[2304,1024]{1,0:T(8,128)(2,1)}) %all-gather.13.cloned.1.call-update) | async-done | bytes 4718608 | tf_op jit(solution)/shard_map/all_gather | solution.py:222
  711.4 3.8 convolution_convert_fusion.6
  716.2 4.9 convolution_convert_fusion.3
  721.9 124.8 %while.28 = (s32[]{:T(128)}, f32[2304,2,64]{0,2,1:T(8,128)S(1)}, f32[2304,2,64]{0,2,1:T(8,128)}, bf16[3,768,2,64]{1,3,2,0:T(8,128)(2,1)}, s32[3]{0:T(128)S(1)}, ...) while((s32[]{:T(128)}, f32[2304,2,64]{0,2,1:T(8,128)S(1)}, ...), condition=%wide.region_18.19_spmd.clone, body=%wide.region_16.18_spmd.clone.sunk | while | flops 2305522944 | bytes 154985072 | solution.py:105
  727.9 8.0 fusion.147
  736.0 8.5 multiply_reduce_fusion.3
  744.5 9.2 multiply_convert_fusion.3
  756.2 6.4 fusion.151
  769.7 8.0 fusion.147
  777.7 8.4 multiply_reduce_fusion.3
  786.1 8.9 multiply_convert_fusion.3
  797.5 6.4 fusion.151
  811.0 8.0 fusion.147
  819.0 8.4 multiply_reduce_fusion.3
  827.4 8.9 multiply_convert_fusion.3
  838.9 6.4 fusion.151
  853.6 4.9 fusion.54
  859.8 6.0 bitcast_convert_fusion
  866.8 6.5 all-reduce.1
  881.2 5.8 all-gather.15.cloned.1.call-done
  893.4 92.7 %reduce-scatter.11.cloned.1.call-done = bf16[288,1024]{1,0:T(8,128)(2,1)} async-done(((bf16[2304,1024]{1,0:T(8,128)(2,1)}), bf16[288,1024]{1,0:T(8,128)(2,1)}) %reduce-scatter.11.cloned.1.call-update) | async-done | bytes 589840 | tf_op jit(solution)/shard_map/reduce_scatter | solution.py:242
  989.7 40.8 %all-reduce = (f32[2,1024]{1,0:T(2,128)}, f32[2,1024]{1,0:T(2,128)}, f32[2,1024]{1,0:T(2,128)}) all-reduce(f32[2,1024]{1,0:T(2,128)S(1)} %pad_maximum_fusion.3, f32[2,1024]{1,0:T(2,128)S(1)} %pad_maximum_fusion.4, f32[2,1024]{1,0:T(2,128)S(1)} %pad_maximum_fusion.5), channel_id=1, replica_groups=mesh['dp'=4,'mp'=8] {'dp','mp'}, use_global_device_ids=true, to_apply=%region_34.35 | all-reduce | flops 6144 | bytes 49152 | tf_op jit(solution)/shard_map/psum | solution.py:253
  (230 shorter events, 87.4 us)
Async XLA Ops:
  7.2 403.8 %copy-start = (bf16[512,1024]{1,0:T(8,128)(2,1)S(1)}, bf16[512,1024]{1,0:T(8,128)(2,1)}, u32[]{:S(2)}) copy-start(bf16[512,1024]{1,0:T(8,128)(2,1)} %param.27) | copy-start | bytes 3145732
  7.2 8.5 copy-start.45
  7.2 8.5 copy-start.46
  7.2 8.6 copy-start.22
  7.2 8.9 copy-start.18
  7.2 9.0 copy-start.42
  7.2 90.5 %all-gather.7.cloned.1.call-start = ((), (), s32[]{:S(2)}) async-start(), calls=%async_computation.4 | async-start | bytes 5308416 | tf_op jit(solution)/shard_map/all_gather | solution.py:146
  8.7 93.5 %copy-start.29 = (f32[288]{0:T(512)}, f32[288]{0:T(512)S(1)}, u32[]{:S(2)}) copy-start(f32[288]{0:T(512)S(1)} %broadcast_multiply_fusion.1) | copy-start | bytes 3460
  10.7 5.6 copy-start.31
  12.0 90.1 %copy-start.26 = (f32[1,1024]{1,0:T(1,128)}, f32[1,1024]{1,0:T(1,128)S(1)}, u32[]{:S(2)}) copy-start(f32[1,1024]{1,0:T(1,128)S(1)} %get-tuple-element.270) | copy-start | bytes 12292
  15.6 231.9 %reduce-scatter.5.cloned.1.call-start = ((), (), s32[]{:S(2)}) async-start(), calls=%async_computation.5 | async-start | bytes 5308416 | tf_op jit(solution)/shard_map/reduce_scatter | solution.py:155
  153.3 94.2 %copy-start.3 = (bf16[288,1024]{1,0:T(8,128)(2,1)S(1)}, bf16[288,1024]{1,0:T(8,128)(2,1)}, u32[]{:S(2)}) copy-start(bf16[288,1024]{1,0:T(8,128)(2,1)} %param.18) | copy-start | bytes 1769476
  153.3 97.0 %copy-start.28 = (f32[1,1024]{1,0:T(1,128)S(1)}, f32[1,1024]{1,0:T(1,128)}, u32[]{:S(2)}) copy-start(f32[1,1024]{1,0:T(1,128)} %get-tuple-element.271) | copy-start | bytes 12292
  153.4 97.0 %copy-start.39 = (f32[1,1024]{1,0:T(1,128)S(1)}, f32[1,1024]{1,0:T(1,128)}, u32[]{:S(2)}) copy-start(f32[1,1024]{1,0:T(1,128)} %get-tuple-element.273) | copy-start | bytes 12292
  153.4 177.3 %all-gather.9.cloned.1.call-start = ((), (), s32[]{:S(2)}) async-start(), calls=%async_computation.6 | async-start | bytes 5308416 | tf_op jit(solution)/shard_map/all_gather | solution.py:164
  250.4 80.3 %copy-start.44 = (f32[512]{0:T(512)S(1)}, f32[512]{0:T(512)}, u32[]{:S(2)}) copy-start(f32[512]{0:T(512)} %param.26) | copy-start | bytes 6148
  251.6 159.4 %all-gather.11.cloned.1.call-start = ((), (), s32[]{:S(2)}) async-start(), calls=%async_computation.8 | async-start | bytes 5308416 | tf_op jit(solution)/shard_map/all_gather | solution.py:204
  253.8 274.3 %reduce-scatter.9.cloned.1.call-start = ((), (), s32[]{:S(2)}) async-start(), calls=%async_computation.9 | async-start | bytes 5308416 | tf_op jit(solution)/shard_map/reduce_scatter | solution.py:211
  411.0 18.4 %copy-start.43 = (bf16[1024,512]{1,0:T(8,128)(2,1)S(1)}, bf16[1024,512]{1,0:T(8,128)(2,1)}, u32[]{:S(2)}) copy-start(bf16[1024,512]{1,0:T(8,128)(2,1)} %param.25) | copy-start | bytes 3145732
  433.9 193.0 %reduce-scatter.7.cloned.1.call-start = ((), (), s32[]{:S(2)}) async-start(), calls=%async_computation.7 | async-start | bytes 5308416 | tf_op jit(solution)/shard_map/reduce_scatter | solution.py:169
  444.7 266.7 %all-gather.13.cloned.1.call-start = ((), (), s32[]{:S(2)}) async-start(), calls=%async_computation.10 | async-start | bytes 5308416 | tf_op jit(solution)/shard_map/all_gather | solution.py:222
  528.1 98.8 %copy-start.15 = (bf16[288,1024]{1,0:T(8,128)(2,1)S(1)}, bf16[288,1024]{1,0:T(8,128)(2,1)}, u32[]{:S(2)}) copy-start(bf16[288,1024]{1,0:T(8,128)(2,1)} %reduce-scatter.9.cloned.1.call-done) | copy-start | bytes 1769476
  632.3 242.6 %all-reduce.5.cloned.1.call-start = ((), (), s32[]{:S(2)}) async-start(), calls=%async_computation.13 | async-start | bytes 4718592 | tf_op jit(solution)/shard_map/psum | solution.py:273
  632.4 6.9 copy-start.20
  639.2 72.2 %copy-start.14 = (bf16[16,8,3,768]{3,1,2,0:T(8,128)(2,1)S(1)}, bf16[16,8,3,768]{3,1,2,0:T(8,128)(2,1)}, u32[]{:S(2)}) copy-start(bf16[16,8,3,768]{3,1,2,0:T(8,128)(2,1)} %copy-done.13) | copy-start | bytes 1769476
  715.3 6.6 copy-start.10
  715.3 171.7 %all-gather.15.cloned.1.call-start = ((), (), s32[]{:S(2)}) async-start(), calls=%async_computation.12 | async-start | bytes 3932160 | tf_op jit(solution)/shard_map/all_gather | solution.py:270
  744.4 9.2 copy-start.5
  756.1 6.5 copy-start.6
  756.2 6.5 copy-start.2
  786.1 8.9 copy-start.5
  797.5 6.4 copy-start.6
  797.5 6.4 copy-start.2
  827.4 8.9 copy-start.5
  838.8 6.4 copy-start.6
  838.8 6.4 copy-start.2
  859.8 126.4 %reduce-scatter.11.cloned.1.call-start = ((), (), s32[]{:S(2)}) async-start(), calls=%async_computation.11 | async-start | bytes 5308416 | tf_op jit(solution)/shard_map/reduce_scatter | solution.py:242
  874.9 4.7 copy-start.21
  889.5 96.6 %copy-start.4 = (bf16[288,1024]{1,0:T(8,128)(2,1)S(1)}, bf16[288,1024]{1,0:T(8,128)(2,1)}, u32[]{:S(2)}) copy-start(bf16[288,1024]{1,0:T(8,128)(2,1)} %param.18) | copy-start | bytes 1769476
  889.6 96.6 %copy-start.27 = (f32[1,1024]{1,0:T(1,128)S(1)}, f32[1,1024]{1,0:T(1,128)}, u32[]{:S(2)}) copy-start(f32[1,1024]{1,0:T(1,128)} %copy-done.26) | copy-start | bytes 12292
  889.6 96.6 %copy-start.30 = (f32[288]{0:T(512)S(1)}, f32[288]{0:T(512)}, u32[]{:S(2)}) copy-start(f32[288]{0:T(512)} %copy-done.29) | copy-start | bytes 3460
  889.6 98.3 %copy-start.34 = (f32[288]{0:T(512)S(1)}, f32[288]{0:T(512)}, u32[]{:S(2)}) copy-start(f32[288]{0:T(512)} %copy-done.33) | copy-start | bytes 3460
  889.6 98.3 %copy-start.32 = (f32[288]{0:T(512)S(1)}, f32[288]{0:T(512)}, u32[]{:S(2)}) copy-start(f32[288]{0:T(512)} %copy-done.31) | copy-start | bytes 3460
  890.8 98.9 %copy-start.35 = (f32[1024]{0:T(1024)S(1)}, f32[1024]{0:T(1024)}, u32[]{:S(2)}) copy-start(f32[1024]{0:T(1024)} %get-tuple-element.198) | copy-start | bytes 12292
  890.8 98.9 %copy-start.36 = (f32[1024]{0:T(1024)S(1)}, f32[1024]{0:T(1024)}, u32[]{:S(2)}) copy-start(f32[1024]{0:T(1024)} %get-tuple-element.192) | copy-start | bytes 12292
  890.8 139.7 %copy-start.12 = (f32[288,1024]{1,0:T(8,128)S(1)}, f32[288,1024]{1,0:T(8,128)}, u32[]{:S(2)}) copy-start(f32[288,1024]{1,0:T(8,128)} %copy-done.11) | copy-start | bytes 3538948
  986.2 44.3 %copy-start.17 = (bf16[288,1024]{1,0:T(8,128)(2,1)S(1)}, bf16[288,1024]{1,0:T(8,128)(2,1)}, u32[]{:S(2)}) copy-start(bf16[288,1024]{1,0:T(8,128)(2,1)} %reduce-scatter.11.cloned.1.call-done) | copy-start | bytes 1769476
  986.2 45.6 %copy-start.1 = (bf16[512,1024]{1,0:T(8,128)(2,1)S(1)}, bf16[512,1024]{1,0:T(8,128)(2,1)}, u32[]{:S(2)}) copy-start(bf16[512,1024]{1,0:T(8,128)(2,1)} %param.27) | copy-start | bytes 3145732
  (16 other events, 29.2 us)
Sparse Core Ops, SparseCore 0:
  15.7 82.0 all-gather.6
  153.5 93.9 reduce-scatter.4
  251.7 78.9 all-gather.8
  333.3 77.6 all-gather.10
  434.0 93.9 reduce-scatter.8
  531.6 95.2 reduce-scatter.6
  632.4 78.9 all-gather.12
  715.4 54.0 all-reduce.4
  859.9 27.0 all-gather.14
  890.5 95.6 reduce-scatter.10
